TPU v7x, 32 devices: a whole 2x2x4 slice. The times are simulated.
32 devices in a mesh: ctx: 8 (over z, x), head: 4 (over y, core).
Axes of the slice: x: 2, y: 2, z: 4, core: 2. Of those that a mesh axis runs over, the one named last changes fastest.
Arguments:
- queries: bfloat16 [2048, 2048], P(('ctx', 'head')), may hold values from -6 to 6
- key_vectors_state: bfloat16 [2048, 512], P(('ctx', 'head')), may hold values from -6 to 6
- value_vectors_state: bfloat16 [2048, 512], P(('ctx', 'head')), may hold values from -6 to 6
- doc_bounds: int32 [17], replicated, may hold values from 0 to 2048, as said below
Outputs:
- attended: bfloat16 [2048, 2048], P(('ctx', 'head'))
Inputs may be any that keep to these rules, and one draw needn't show every extreme that they name: doc_bounds[0] is 0 and doc_bounds[16] is 2048; the entries strictly increase, and doc_bounds[1] to doc_bounds[15] all lie below 1024, so the last document holds at least half of the tokens.
All inputs are finite; a program needn't handle non-finite values.
Results may differ from a plain program's by a relative error of at most 0.004.
Values may be sent and summed in bfloat16 or wider, within the bound.
A program may use at most 64 MiB of HBM per device.

v0:
```python
import math
import jax
import jax.numpy as jnp
from jax import lax
from jax.sharding import PartitionSpec as P

QUERY_HEADS = 32
KEY_VALUE_HEADS = 8
HEAD_SIZE = 64
masked_score = -1e30


def from_behind(block, axis, distance):
    devices = range(lax.axis_size(axis))
    route = [((i - distance) % len(devices), i) for i in devices]
    return lax.ppermute(block, axis, route)


def document_of(positions, doc_bounds):
    interior = doc_bounds[1:-1]
    return jnp.sum((interior[None, :] <= positions[:, None]).astype(jnp.int32), axis=1)


def on_device(queries, key_vectors_state, value_vectors_state, doc_bounds):
    query_loc, key_loc, value_loc = (
        lax.all_to_all(queries, "head", split_axis=1, concat_axis=0, tiled=True),
        lax.all_to_all(key_vectors_state, "head", split_axis=1, concat_axis=0, tiled=True),
        lax.all_to_all(value_vectors_state, "head", split_axis=1, concat_axis=0, tiled=True),
    )
    tok_rows = query_loc.shape[0]
    cycle_size = lax.axis_size("ctx")
    my_index = lax.axis_index("ctx")
    kv_local = key_loc.shape[1] // HEAD_SIZE
    queries_per_group = QUERY_HEADS // KEY_VALUE_HEADS
    score_scale = 1.0 / math.sqrt(HEAD_SIZE)
    first_pos = my_index * tok_rows
    query_pos = first_pos + jnp.arange(tok_rows, dtype=jnp.int32)
    heads_of_queries = query_loc.reshape(tok_rows, kv_local, queries_per_group, HEAD_SIZE)
    query_doc = document_of(query_pos, doc_bounds)

    def attend(running, key_piece, value_piece, anchor):
        key_count = key_piece.shape[0]
        key_pos = anchor + jnp.arange(key_count, dtype=jnp.int32)
        key_doc = document_of(key_pos, doc_bounds)
        allowed = (
            (query_doc[:, None] == key_doc[None, :])
            & (key_pos[None, :] <= query_pos[:, None])
            & (key_pos[None, :] >= 0)
        )
        heads_of_keys = key_piece.reshape(key_count, kv_local, HEAD_SIZE)
        heads_of_values = value_piece.reshape(key_count, kv_local, HEAD_SIZE)
        run_max, run_sum, weighted = running
        scores = (
            jnp.einsum(
                "qgjd,kgd->qgjk",
                heads_of_queries,
                heads_of_keys,
                preferred_element_type=jnp.float32,
            )
            * score_scale
        )
        visible = allowed[:, None, None, :]
        masked = jnp.where(visible, scores, masked_score)
        new_max = jnp.maximum(run_max, jnp.max(masked, axis=-1))
        weights = jnp.exp(masked - new_max[..., None]) * visible.astype(jnp.float32)
        shrink = jnp.exp(run_max - new_max)
        new_sum = run_sum * shrink + jnp.sum(weights, axis=-1)
        rounded = weights.astype(jnp.bfloat16)
        mixed = jnp.einsum(
            "qgjk,kgd->qgjd", rounded, heads_of_values, preferred_element_type=jnp.float32
        )
        return (new_max, new_sum, weighted * shrink[..., None] + mixed)

    def fold_keys(running, key_piece, value_piece, anchor):
        key_count = key_piece.shape[0]
        return attend(running, key_piece, value_piece, anchor)

    stat_shape = (tok_rows, kv_local, queries_per_group)
    initial = (
        jnp.full(stat_shape, masked_score, jnp.float32),
        jnp.zeros(stat_shape, jnp.float32),
        jnp.zeros((tok_rows, kv_local, queries_per_group, HEAD_SIZE), jnp.float32),
    )
    bound_heads = doc_bounds[:-1]
    doc_start = jnp.max(
        jnp.where(bound_heads[None, :] <= query_pos[:, None], bound_heads[None, :], 0), axis=1
    )
    start_block = doc_start // tok_rows
    own_block = query_pos // tok_rows
    row_turns = jnp.where(
        own_block <= my_index,
        my_index - start_block,
        jnp.where(start_block <= my_index, cycle_size - 1, my_index - start_block + cycle_size),
    )
    reach_steps = lax.pmax(jnp.max(row_turns), "ctx")
    running = fold_keys(initial, key_loc, value_loc, first_pos)

    def cycle_turn(turn_index, state):
        paired, inner_state = state
        paired = from_behind(paired, "ctx", 1)
        anchor = jnp.mod(my_index - turn_index - 1, cycle_size) * tok_rows
        return (paired, fold_keys(inner_state, paired[0], paired[1], anchor))

    stacked = jnp.stack((key_loc, value_loc))
    stacked, running = lax.fori_loop(0, reach_steps, cycle_turn, (stacked, running))
    run_max, run_sum, weighted = running
    attended = (
        (weighted / run_sum[..., None])
        .astype(jnp.bfloat16)
        .reshape(tok_rows, kv_local * queries_per_group * HEAD_SIZE)
    )
    return lax.all_to_all(attended, "head", split_axis=0, concat_axis=1, tiled=True)


def solution(mesh):
    return jax.shard_map(
        on_device,
        mesh=mesh,
        in_specs=(
            P(("ctx", "head"), None),
            P(("ctx", "head"), None),
            P(("ctx", "head"), None),
            P(),
        ),
        out_specs=P(("ctx", "head"), None),
        check_vma=False,
    )
```

profile of v0, /device:TPU:0, one launch (start us, length us, event | category | flops | bytes accessed | tf_op | source)
XLA Modules:
  0.0 87.6 jit_solution(5063558174066637305)
XLA Ops:
  0.0 0.8 copy-done
  0.8 0.6 copy_bitcast_fusion.2
  1.5 4.3 %all-to-all-start = ((bf16[64,4,128]{2,0,1:T(8,128)(2,1)}), bf16[64,4,128]{2,0,1:T(8,128)(2,1)S(1)}, u32[]{:S(2)}, u32[]{:S(2)}) async-start(bf16[64,4,128]{2,0,1:T(8,128)(2,1)} %copy_bitcast_fusion.2), calls=%async_computation | async-start | bytes 131072 | tf_op jit(solution)/shard_map/all_to_all | solution.py:27
  5.7 0.7 slice.25
  6.6 0.7 select_reduce_fusion
  7.3 1.5 %copy_bitcast_fusion.1 = bf16[64,4,128]{2,0,1:T(8,128)(2,1)} fusion(bf16[64,512]{1,0:T(8,128)(2,1)} %param.8), kind=kLoop, calls=%fused_computation.40 | loop fusion | bytes 131072 | tf_op jit(solution)/shard_map/all_to_all | solution.py:28
  9.9 3.3 %all-to-all-start.1 = ((bf16[64,4,128]{2,0,1:T(8,128)(2,1)}), bf16[64,4,128]{2,0,1:T(8,128)(2,1)S(1)}, u32[]{:S(2)}, u32[]{:S(2)}) async-start(bf16[64,4,128]{2,0,1:T(8,128)(2,1)} %copy_bitcast_fusion.1), calls=%async_computation.1 | async-start | bytes 131072 | tf_op jit(solution)/shard_map/all_to_all | solution.py:28
  13.2 1.7 %copy.82 = bf16[8,4,8,512]{3,2,0,1:T(8,128)(2,1)} copy(bf16[8,4,8,512]{3,2,1,0:T(8,128)(2,1)} %bitcast.126) | data formatting | bytes 524288 | tf_op jit(solution)/shard_map/all_to_all | solution.py:26
  14.8 2.4 %all-to-all-done.1 = bf16[64,4,128]{2,0,1:T(8,128)(2,1)S(1)} async-done(((bf16[64,4,128]{2,0,1:T(8,128)(2,1)}), bf16[64,4,128]{2,0,1:T(8,128)(2,1)S(1)}, u32[]{:S(2)}, u32[]{:S(2)}) %all-to-all-start.1) | async-done | bytes 65568 | tf_op jit(solution)/shard_map/all_to_all | solution.py:28
  17.2 3.4 %all-to-all-start.2 = ((bf16[64,4,512]{2,0,1:T(8,128)(2,1)}), bf16[64,4,512]{2,0,1:T(8,128)(2,1)S(1)}, u32[]{:S(2)}, u32[]{:S(2)}) async-start(bf16[64,4,512]{2,0,1:T(8,128)(2,1)} %bitcast.73), calls=%async_computation.2 | async-start | bytes 524288 | tf_op jit(solution)/shard_map/all_to_all | solution.py:26
  20.8 12.6 %pmax.7 = s32[]{:T(128)} all-reduce(s32[]{:T(128)} %fusion.26), channel_id=1, replica_groups=mesh['ctx'=8,'head'=4] {'ctx'}, use_global_device_ids=true, to_apply=%region_5.6 | all-reduce | flops 1 | bytes 8 | tf_op jit(solution)/shard_map/pmax | solution.py:95
  35.4 0.7 fusion.17
  36.2 41.1 %while.19 = (s32[]{:T(128)}, bf16[2,256,128]{1,2,0:T(8,128)(2,1)S(1)}, f32[256,2,4]{0,2,1:T(4,128)S(1)}, f32[256,2,4]{0,2,1:T(4,128)S(1)}, f32[256,2,4,64]{0,3,2...) while((s32[]{:T(128)}, ...), condition=%wide.region_10.11_spmd.clone, body=%wide.region_6.10_spmd.clone.sunk | while | flops 141639696 | bytes 9970710 | solution.py:105
  36.7 1.5 %collective-permute-start = (bf16[2,256,128]{1,2,0:T(8,128)(2,1)S(1)}, bf16[2,256,128]{1,2,0:T(8,128)(2,1)S(1)}, u32[]{:S(2)}, u32[]{:S(2)}) collective-permute-start(bf16[2,256,128]{1,2,0:T(8,128)(2,1)S(1)} %get-tuple-element.362), channel_id=1, source_target_pairs={{28,0},{0,4},{4,8},{8,12},{12,16},{16,20},{20,24},{24,28},{29,1},{... | collective-permute-start | bytes 393224 | tf_op jit(solution)/shard_map/while/body/ppermute | solution.py:16
  38.7 5.8 %collective-permute-done = bf16[2,256,128]{1,2,0:T(8,128)(2,1)S(1)} collective-permute-done((bf16[2,256,128]{1,2,0:T(8,128)(2,1)S(1)}, bf16[2,256,128]{1,2,0:T(8,128)(2,1)S(1)}, u32[]{:S(2)}, u32[]{:S(2)}) %collective-permute-start) | collective-permute-done | bytes 131104 | tf_op jit(solution)/shard_map/while/body/ppermute | solution.py:16
  45.5 0.7 fusion.56
  47.3 7.3 %collective-permute-done = bf16[2,256,128]{1,2,0:T(8,128)(2,1)S(1)} collective-permute-done((bf16[2,256,128]{1,2,0:T(8,128)(2,1)S(1)}, bf16[2,256,128]{1,2,0:T(8,128)(2,1)S(1)}, u32[]{:S(2)}, u32[]{:S(2)}) %collective-permute-start) | collective-permute-done | bytes 131104 | tf_op jit(solution)/shard_map/while/body/ppermute | solution.py:16
  55.7 0.7 fusion.56
  57.5 7.3 %collective-permute-done = bf16[2,256,128]{1,2,0:T(8,128)(2,1)S(1)} collective-permute-done((bf16[2,256,128]{1,2,0:T(8,128)(2,1)S(1)}, bf16[2,256,128]{1,2,0:T(8,128)(2,1)S(1)}, u32[]{:S(2)}, u32[]{:S(2)}) %collective-permute-start) | collective-permute-done | bytes 131104 | tf_op jit(solution)/shard_map/while/body/ppermute | solution.py:16
  65.8 0.7 fusion.56
  67.6 7.3 %collective-permute-done = bf16[2,256,128]{1,2,0:T(8,128)(2,1)S(1)} collective-permute-done((bf16[2,256,128]{1,2,0:T(8,128)(2,1)S(1)}, bf16[2,256,128]{1,2,0:T(8,128)(2,1)S(1)}, u32[]{:S(2)}, u32[]{:S(2)}) %collective-permute-start) | collective-permute-done | bytes 131104 | tf_op jit(solution)/shard_map/while/body/ppermute | solution.py:16
  75.9 0.7 fusion.56
  77.9 9.1 %all_to_all.67 = bf16[4,64,512]{2,1,0:T(8,128)(2,1)S(1)} all-to-all(bf16[4,64,512]{2,1,0:T(8,128)(2,1)S(1)} %copy.68), channel_id=1, replica_groups=mesh['ctx'=8,'head'=4] {'head'}, dimensions={0} | all-to-all | bytes 524288 | tf_op jit(solution)/shard_map/all_to_all | solution.py:112
  86.9 0.7 copy.72
  (78 shorter events, 9.7 us)
Async XLA Ops:
  0.0 0.8 copy-start
  1.5 8.4 %all-to-all-start = ((bf16[64,4,128]{2,0,1:T(8,128)(2,1)}), bf16[64,4,128]{2,0,1:T(8,128)(2,1)S(1)}, u32[]{:S(2)}, u32[]{:S(2)}) async-start(bf16[64,4,128]{2,0,1:T(8,128)(2,1)} %copy_bitcast_fusion.2), calls=%async_computation | async-start | bytes 131072 | tf_op jit(solution)/shard_map/all_to_all | solution.py:27
  9.9 7.4 %all-to-all-start.1 = ((bf16[64,4,128]{2,0,1:T(8,128)(2,1)}), bf16[64,4,128]{2,0,1:T(8,128)(2,1)S(1)}, u32[]{:S(2)}, u32[]{:S(2)}) async-start(bf16[64,4,128]{2,0,1:T(8,128)(2,1)} %copy_bitcast_fusion.1), calls=%async_computation.1 | async-start | bytes 131072 | tf_op jit(solution)/shard_map/all_to_all | solution.py:28
  17.2 16.5 %all-to-all-start.2 = ((bf16[64,4,512]{2,0,1:T(8,128)(2,1)}), bf16[64,4,512]{2,0,1:T(8,128)(2,1)S(1)}, u32[]{:S(2)}, u32[]{:S(2)}) async-start(bf16[64,4,512]{2,0,1:T(8,128)(2,1)} %bitcast.73), calls=%async_computation.2 | async-start | bytes 524288 | tf_op jit(solution)/shard_map/all_to_all | solution.py:26
  35.4 0.8 copy-start.1
  36.7 7.7 %collective-permute-start = (bf16[2,256,128]{1,2,0:T(8,128)(2,1)S(1)}, bf16[2,256,128]{1,2,0:T(8,128)(2,1)S(1)}, u32[]{:S(2)}, u32[]{:S(2)}) collective-permute-start(bf16[2,256,128]{1,2,0:T(8,128)(2,1)S(1)} %get-tuple-element.362), channel_id=1, source_target_pairs={{28,0},{0,4},{4,8},{8,12},{12,16},{16,20},{20,24},{24,28},{29,1},{... | collective-permute-start | bytes 393224 | tf_op jit(solution)/shard_map/while/body/ppermute | solution.py:16
  46.9 7.7 %collective-permute-start = (bf16[2,256,128]{1,2,0:T(8,128)(2,1)S(1)}, bf16[2,256,128]{1,2,0:T(8,128)(2,1)S(1)}, u32[]{:S(2)}, u32[]{:S(2)}) collective-permute-start(bf16[2,256,128]{1,2,0:T(8,128)(2,1)S(1)} %get-tuple-element.362), channel_id=1, source_target_pairs={{28,0},{0,4},{4,8},{8,12},{12,16},{16,20},{20,24},{24,28},{29,1},{... | collective-permute-start | bytes 393224 | tf_op jit(solution)/shard_map/while/body/ppermute | solution.py:16
  57.0 7.7 %collective-permute-start = (bf16[2,256,128]{1,2,0:T(8,128)(2,1)S(1)}, bf16[2,256,128]{1,2,0:T(8,128)(2,1)S(1)}, u32[]{:S(2)}, u32[]{:S(2)}) collective-permute-start(bf16[2,256,128]{1,2,0:T(8,128)(2,1)S(1)} %get-tuple-element.362), channel_id=1, source_target_pairs={{28,0},{0,4},{4,8},{8,12},{12,16},{16,20},{20,24},{24,28},{29,1},{... | collective-permute-start | bytes 393224 | tf_op jit(solution)/shard_map/while/body/ppermute | solution.py:16
  67.1 7.7 %collective-permute-start = (bf16[2,256,128]{1,2,0:T(8,128)(2,1)S(1)}, bf16[2,256,128]{1,2,0:T(8,128)(2,1)S(1)}, u32[]{:S(2)}, u32[]{:S(2)}) collective-permute-start(bf16[2,256,128]{1,2,0:T(8,128)(2,1)S(1)} %get-tuple-element.362), channel_id=1, source_target_pairs={{28,0},{0,4},{4,8},{8,12},{12,16},{16,20},{20,24},{24,28},{29,1},{... | collective-permute-start | bytes 393224 | tf_op jit(solution)/shard_map/while/body/ppermute | solution.py:16
where the time goes:
time: 88.2 us; the launch traced here: 87.6 us
  waiting for transfers between devices  30.4 us (34%)
  blocking collectives  21.7 us (25%)
  starting transfers between devices  12.7 us (14%)
  local copies, waits for them, and re-layouts  7.91 us (9%)
  matrix products  6.12 us (7%)
  other arithmetic  5.49 us (6%)
  loops' own time  3.19 us (4%)
    ppermute x4, waiting for transfers between devices, from_behind(): return lax.ppermute(block, axis, route)  27.6 us
    pmax x1, blocking collectives, on_device(): reach_steps = lax.pmax(jnp.max(row_turns), 'ctx')  12.6 us
    all_to_all x1, blocking collectives, on_device(): lax.all_to_all(attended, 'head', split_axis=0, concat_axis=1, tiled=True)  9.06 us
    all_to_all x1, starting transfers between devices, on_device(): lax.all_to_all(key_vectors_state, 'head', split_axis=1, concat_axis=0, ti...  4.26 us
    dot_general x5, matrix products, attend(): jnp.einsum('qgjk,kgd->qgjd', rounded, heads_of_values, preferred_element_...  3.68 us
    all_to_all x1, starting transfers between devices, on_device(): lax.all_to_all(queries, 'head', split_axis=1, concat_axis=0, tiled=True)  3.41 us
    all_to_all x1, starting transfers between devices, on_device(): lax.all_to_all(value_vectors_state, 'head', split_axis=1, concat_axis=0,...  3.28 us
    another operation x1, loops' own time, on_device(): lax.fori_loop(0, reach_steps, cycle_turn, (stacked, running))  3.19 us
  transfers between devices with their start and end apart: 7, of which 6 were waited for; matrix products, arithmetic and copies ran while one was open for 8% of the time, Pallas kernels for 0%

commit v1 on v0

--- a/solution.py
+++ b/solution.py
@@ -8,6 +8,18 @@
 KEY_VALUE_HEADS = 8
 HEAD_SIZE = 64
 masked_score = -1e30
+
+
+def exchange_directly(value, axis, split, join):
+    ways, here = (lax.axis_size(axis), lax.axis_index(axis))
+    width = value.shape[split] // ways
+    turned = jnp.roll(value, -here * width, axis=split)
+    got = [lax.slice_in_dim(turned, 0, width, axis=split)]
+    for far in range(1, ways):
+        sent = lax.slice_in_dim(turned, far * width, (far + 1) * width, axis=split)
+        got.append(lax.ppermute(sent, axis, [(d, (d + far) % ways) for d in range(ways)]))
+    line = jnp.concatenate(got[::-1], axis=join)
+    return jnp.roll(line, (here + 1) * got[0].shape[join], axis=join)
 
 
 def from_behind(block, axis, distance):
@@ -23,7 +35,7 @@
 
 def on_device(queries, key_vectors_state, value_vectors_state, doc_bounds):
     query_loc, key_loc, value_loc = (
-        lax.all_to_all(queries, "head", split_axis=1, concat_axis=0, tiled=True),
+        exchange_directly(queries, "head", 1, 0),
         lax.all_to_all(key_vectors_state, "head", split_axis=1, concat_axis=0, tiled=True),
         lax.all_to_all(value_vectors_state, "head", split_axis=1, concat_axis=0, tiled=True),
     )

time: 88.2 us -> 84.6 us (0.959)
  waiting for transfers between devices: 30.4 us -> 27.6 us
  local copies, waits for them, and re-layouts: 7.91 us -> 5.86 us
  other arithmetic: 5.49 us -> 6.55 us
    ppermute x0 -> x3, starting transfers between devices: none -> 3.58 us  [exchange_directly(): lax.ppermute(sent, axis, [(d, (d + far) % ways) for d in range(ways)])]
    all_to_all x1 -> x0, starting transfers between devices: 3.41 us -> none  [on_device(): lax.all_to_all(queries, 'head', split_axis=1, concat_axis=0, tiled=True)]
    all_to_all x1, waiting for transfers between devices: 2.4 us -> 0.01 us  [on_device(): lax.all_to_all(value_vectors_state, 'head', split_axis=1, concat_axis=0,...]
    all_to_all x1 -> x0, local copies, waits for them, and re-layouts: 1.68 us -> none  [on_device(): lax.all_to_all(queries, 'head', split_axis=1, concat_axis=0, tiled=True)]
    concatenate x0 -> x1, other arithmetic: none -> 1.06 us  [exchange_directly(): turned = jnp.roll(value, -here * width, axis=split)]
    all_to_all x1, starting transfers between devices: 3.28 us -> 4.26 us  [on_device(): lax.all_to_all(value_vectors_state, 'head', split_axis=1, concat_axis=0,...]
    all_to_all x1, starting transfers between devices: 4.26 us -> 3.29 us  [on_device(): lax.all_to_all(key_vectors_state, 'head', split_axis=1, concat_axis=0, ti...]
  transfers between devices with their start and end apart: 7 -> 9, of which waited for: 6 -> 4; matrix products, arithmetic and copies ran while one was open for 8% -> 8% of each run, Pallas kernels for 0% -> 0%
where the time goes in v1:
time: 84.6 us; the launch traced here: 84.1 us
  waiting for transfers between devices  27.6 us (33%)
  blocking collectives  21.6 us (26%)
  starting transfers between devices  12.9 us (15%)
  other arithmetic  6.55 us (8%)
  matrix products  6.12 us (7%)
  local copies, waits for them, and re-layouts  5.86 us (7%)
  loops' own time  3.19 us (4%)
    ppermute x4, waiting for transfers between devices, from_behind(): return lax.ppermute(block, axis, route)  27.6 us
    pmax x1, blocking collectives, on_device(): reach_steps = lax.pmax(jnp.max(row_turns), 'ctx')  12.6 us
    all_to_all x1, blocking collectives, on_device(): lax.all_to_all(attended, 'head', split_axis=0, concat_axis=1, tiled=True)  9.06 us
    all_to_all x1, starting transfers between devices, on_device(): lax.all_to_all(value_vectors_state, 'head', split_axis=1, concat_axis=0,...  4.26 us
    dot_general x5, matrix products, attend(): jnp.einsum('qgjk,kgd->qgjd', rounded, heads_of_values, preferred_element_...  3.68 us
    ppermute x3, starting transfers between devices, exchange_directly(): lax.ppermute(sent, axis, [(d, (d + far) % ways) for d in range(ways)])  3.58 us
    all_to_all x1, starting transfers between devices, on_device(): lax.all_to_all(key_vectors_state, 'head', split_axis=1, concat_axis=0, ti...  3.29 us
    another operation x1, loops' own time, on_device(): lax.fori_loop(0, reach_steps, cycle_turn, (stacked, running))  3.19 us
  transfers between devices with their start and end apart: 9, of which 4 were waited for; matrix products, arithmetic and copies ran while one was open for 8% of the time, Pallas kernels for 0%

profile of v1, /device:TPU:0, one launch (start us, length us, event | category | flops | bytes accessed | tf_op | source)
XLA Modules:
  0.0 84.1 jit_solution(15840380650065122728)
XLA Ops:
  0.0 0.8 copy-done
  0.8 0.6 copy_bitcast_fusion
  1.5 4.3 %all-to-all-start.1 = ((bf16[64,4,128]{2,0,1:T(8,128)(2,1)}), bf16[64,4,128]{2,0,1:T(8,128)(2,1)S(1)}, u32[]{:S(2)}, u32[]{:S(2)}) async-start(bf16[64,4,128]{2,0,1:T(8,128)(2,1)} %copy_bitcast_fusion), calls=%async_computation.1 | async-start | bytes 131072 | tf_op jit(solution)/shard_map/all_to_all | solution.py:40
  5.7 1.1 %fusion.24 = bf16[64,2048]{1,0:T(8,128)(2,1)S(1)} fusion(s32[]{:T(128)S(6)} %select_n.69, bf16[64,2048]{1,0:T(8,128)(2,1)} %param.6), kind=kLoop, calls=%fused_computation.38 | loop fusion | flops 524288 | bytes 524292 | tf_op jit(solution)/shard_map/jit(_roll_dynamic)/concatenate | solution.py:16
  7.4 1.7 %collective-permute-start.2 = (bf16[64,512]{1,0:T(8,128)(2,1)S(1)}, bf16[64,512]{1,0:T(8,128)(2,1)S(1)}, u32[]{:S(2)}, u32[]{:S(2)}) collective-permute-start(bf16[64,512]{1,0:T(8,128)(2,1)S(1)} %get-tuple-element.251), channel_id=1, source_target_pairs={{0,2},{1,3},{2,0},{3,1},{4,6},{5,7},{6,4},{7,5},{8,10},{9,11},{10,... | collective-permute-start | bytes 196616 | tf_op jit(solution)/shard_map/ppermute | solution.py:20
  9.0 1.4 %collective-permute-start.1 = (bf16[64,512]{1,0:T(8,128)(2,1)S(1)}, bf16[64,512]{1,0:T(8,128)(2,1)S(1)}, u32[]{:S(2)}, u32[]{:S(2)}) collective-permute-start(bf16[64,512]{1,0:T(8,128)(2,1)S(1)} %get-tuple-element.252), channel_id=1, source_target_pairs={{0,3},{1,0},{2,1},{3,2},{4,7},{5,4},{6,5},{7,6},{8,11},{9,8},{10,9... | collective-permute-start | bytes 196616 | tf_op jit(solution)/shard_map/ppermute | solution.py:20
  10.4 0.7 slice.37
  11.2 0.7 select_reduce_fusion
  12.6 1.5 %copy_bitcast_fusion.1 = bf16[64,4,128]{2,0,1:T(8,128)(2,1)} fusion(bf16[64,512]{1,0:T(8,128)(2,1)} %param.7), kind=kLoop, calls=%fused_computation.45 | loop fusion | bytes 131072 | tf_op jit(solution)/shard_map/all_to_all | solution.py:39
  14.1 3.3 %all-to-all-start = ((bf16[64,4,128]{2,0,1:T(8,128)(2,1)}), bf16[64,4,128]{2,0,1:T(8,128)(2,1)S(1)}, u32[]{:S(2)}, u32[]{:S(2)}) async-start(bf16[64,4,128]{2,0,1:T(8,128)(2,1)} %copy_bitcast_fusion.1), calls=%async_computation | async-start | bytes 131072 | tf_op jit(solution)/shard_map/all_to_all | solution.py:39
  17.6 12.6 %pmax.7 = s32[]{:T(128)} all-reduce(s32[]{:T(128)} %fusion.28), channel_id=1, replica_groups=mesh['ctx'=8,'head'=4] {'ctx'}, use_global_device_ids=true, to_apply=%region_5.6 | all-reduce | flops 1 | bytes 8 | tf_op jit(solution)/shard_map/pmax | solution.py:107
  31.8 0.7 fusion.18
  32.6 41.1 %while.19 = (s32[]{:T(128)}, bf16[2,256,128]{1,2,0:T(8,128)(2,1)S(1)}, f32[256,2,4]{0,2,1:T(4,128)S(1)}, f32[256,2,4]{0,2,1:T(4,128)S(1)}, f32[256,2,4,64]{0,3,2...) while((s32[]{:T(128)}, ...), condition=%wide.region_10.11_spmd.clone, body=%wide.region_6.10_spmd.clone.sunk | while | flops 141639696 | bytes 9970710 | solution.py:117
  33.2 1.6 %collective-permute-start = (bf16[2,256,128]{1,2,0:T(8,128)(2,1)S(1)}, bf16[2,256,128]{1,2,0:T(8,128)(2,1)S(1)}, u32[]{:S(2)}, u32[]{:S(2)}) collective-permute-start(bf16[2,256,128]{1,2,0:T(8,128)(2,1)S(1)} %get-tuple-element.365), channel_id=1, source_target_pairs={{28,0},{0,4},{4,8},{8,12},{12,16},{16,20},{20,24},{24,28},{29,1},{... | collective-permute-start | bytes 393224 | tf_op jit(solution)/shard_map/while/body/ppermute | solution.py:28
  35.1 5.8 %collective-permute-done = bf16[2,256,128]{1,2,0:T(8,128)(2,1)S(1)} collective-permute-done((bf16[2,256,128]{1,2,0:T(8,128)(2,1)S(1)}, bf16[2,256,128]{1,2,0:T(8,128)(2,1)S(1)}, u32[]{:S(2)}, u32[]{:S(2)}) %collective-permute-start) | collective-permute-done | bytes 131104 | tf_op jit(solution)/shard_map/while/body/ppermute | solution.py:28
  42.0 0.7 fusion.59
  43.7 7.3 %collective-permute-done = bf16[2,256,128]{1,2,0:T(8,128)(2,1)S(1)} collective-permute-done((bf16[2,256,128]{1,2,0:T(8,128)(2,1)S(1)}, bf16[2,256,128]{1,2,0:T(8,128)(2,1)S(1)}, u32[]{:S(2)}, u32[]{:S(2)}) %collective-permute-start) | collective-permute-done | bytes 131104 | tf_op jit(solution)/shard_map/while/body/ppermute | solution.py:28
  52.1 0.7 fusion.59
  53.9 7.3 %collective-permute-done = bf16[2,256,128]{1,2,0:T(8,128)(2,1)S(1)} collective-permute-done((bf16[2,256,128]{1,2,0:T(8,128)(2,1)S(1)}, bf16[2,256,128]{1,2,0:T(8,128)(2,1)S(1)}, u32[]{:S(2)}, u32[]{:S(2)}) %collective-permute-start) | collective-permute-done | bytes 131104 | tf_op jit(solution)/shard_map/while/body/ppermute | solution.py:28
  62.2 0.7 fusion.59
  64.0 7.3 %collective-permute-done = bf16[2,256,128]{1,2,0:T(8,128)(2,1)S(1)} collective-permute-done((bf16[2,256,128]{1,2,0:T(8,128)(2,1)S(1)}, bf16[2,256,128]{1,2,0:T(8,128)(2,1)S(1)}, u32[]{:S(2)}, u32[]{:S(2)}) %collective-permute-start) | collective-permute-done | bytes 131104 | tf_op jit(solution)/shard_map/while/body/ppermute | solution.py:28
  72.3 0.7 fusion.59
  74.3 9.1 %all_to_all.51 = bf16[4,64,512]{2,1,0:T(8,128)(2,1)S(1)} all-to-all(bf16[4,64,512]{2,1,0:T(8,128)(2,1)S(1)} %copy.60), channel_id=1, replica_groups=mesh['ctx'=8,'head'=4] {'head'}, dimensions={0} | all-to-all | bytes 524288 | tf_op jit(solution)/shard_map/all_to_all | solution.py:124
  83.3 0.7 copy.63
  (91 shorter events, 9.4 us)
Async XLA Ops:
  0.0 0.8 copy-start
  1.5 12.6 %all-to-all-start.1 = ((bf16[64,4,128]{2,0,1:T(8,128)(2,1)}), bf16[64,4,128]{2,0,1:T(8,128)(2,1)S(1)}, u32[]{:S(2)}, u32[]{:S(2)}) async-start(bf16[64,4,128]{2,0,1:T(8,128)(2,1)} %copy_bitcast_fusion), calls=%async_computation.1 | async-start | bytes 131072 | tf_op jit(solution)/shard_map/all_to_all | solution.py:40
  6.8 23.7 %collective-permute-start.3 = (bf16[64,512]{1,0:T(8,128)(2,1)S(1)}, bf16[64,512]{1,0:T(8,128)(2,1)S(1)}, u32[]{:S(2)}, u32[]{:S(2)}) collective-permute-start(bf16[64,512]{1,0:T(8,128)(2,1)S(1)} %get-tuple-element.250), channel_id=1, source_target_pairs={{0,1},{1,2},{2,3},{3,0},{4,5},{5,6},{6,7},{7,4},{8,9},{9,10},{10,1... | collective-permute-start | bytes 196616 | tf_op jit(solution)/shard_map/ppermute | solution.py:20
  7.4 23.2 %collective-permute-start.2 = (bf16[64,512]{1,0:T(8,128)(2,1)S(1)}, bf16[64,512]{1,0:T(8,128)(2,1)S(1)}, u32[]{:S(2)}, u32[]{:S(2)}) collective-permute-start(bf16[64,512]{1,0:T(8,128)(2,1)S(1)} %get-tuple-element.251), channel_id=1, source_target_pairs={{0,2},{1,3},{2,0},{3,1},{4,6},{5,7},{6,4},{7,5},{8,10},{9,11},{10,... | collective-permute-start | bytes 196616 | tf_op jit(solution)/shard_map/ppermute | solution.py:20
  9.0 21.5 %collective-permute-start.1 = (bf16[64,512]{1,0:T(8,128)(2,1)S(1)}, bf16[64,512]{1,0:T(8,128)(2,1)S(1)}, u32[]{:S(2)}, u32[]{:S(2)}) collective-permute-start(bf16[64,512]{1,0:T(8,128)(2,1)S(1)} %get-tuple-element.252), channel_id=1, source_target_pairs={{0,3},{1,0},{2,1},{3,2},{4,7},{5,4},{6,5},{7,6},{8,11},{9,8},{10,9... | collective-permute-start | bytes 196616 | tf_op jit(solution)/shard_map/ppermute | solution.py:20
  14.1 16.2 %all-to-all-start = ((bf16[64,4,128]{2,0,1:T(8,128)(2,1)}), bf16[64,4,128]{2,0,1:T(8,128)(2,1)S(1)}, u32[]{:S(2)}, u32[]{:S(2)}) async-start(bf16[64,4,128]{2,0,1:T(8,128)(2,1)} %copy_bitcast_fusion.1), calls=%async_computation | async-start | bytes 131072 | tf_op jit(solution)/shard_map/all_to_all | solution.py:39
  31.8 0.8 copy-start.1
  33.2 7.7 %collective-permute-start = (bf16[2,256,128]{1,2,0:T(8,128)(2,1)S(1)}, bf16[2,256,128]{1,2,0:T(8,128)(2,1)S(1)}, u32[]{:S(2)}, u32[]{:S(2)}) collective-permute-start(bf16[2,256,128]{1,2,0:T(8,128)(2,1)S(1)} %get-tuple-element.365), channel_id=1, source_target_pairs={{28,0},{0,4},{4,8},{8,12},{12,16},{16,20},{20,24},{24,28},{29,1},{... | collective-permute-start | bytes 393224 | tf_op jit(solution)/shard_map/while/body/ppermute | solution.py:28
  43.3 7.7 %collective-permute-start = (bf16[2,256,128]{1,2,0:T(8,128)(2,1)S(1)}, bf16[2,256,128]{1,2,0:T(8,128)(2,1)S(1)}, u32[]{:S(2)}, u32[]{:S(2)}) collective-permute-start(bf16[2,256,128]{1,2,0:T(8,128)(2,1)S(1)} %get-tuple-element.365), channel_id=1, source_target_pairs={{28,0},{0,4},{4,8},{8,12},{12,16},{16,20},{20,24},{24,28},{29,1},{... | collective-permute-start | bytes 393224 | tf_op jit(solution)/shard_map/while/body/ppermute | solution.py:28
  53.4 7.7 %collective-permute-start = (bf16[2,256,128]{1,2,0:T(8,128)(2,1)S(1)}, bf16[2,256,128]{1,2,0:T(8,128)(2,1)S(1)}, u32[]{:S(2)}, u32[]{:S(2)}) collective-permute-start(bf16[2,256,128]{1,2,0:T(8,128)(2,1)S(1)} %get-tuple-element.365), channel_id=1, source_target_pairs={{28,0},{0,4},{4,8},{8,12},{12,16},{16,20},{20,24},{24,28},{29,1},{... | collective-permute-start | bytes 393224 | tf_op jit(solution)/shard_map/while/body/ppermute | solution.py:28
  63.5 7.7 %collective-permute-start = (bf16[2,256,128]{1,2,0:T(8,128)(2,1)S(1)}, bf16[2,256,128]{1,2,0:T(8,128)(2,1)S(1)}, u32[]{:S(2)}, u32[]{:S(2)}) collective-permute-start(bf16[2,256,128]{1,2,0:T(8,128)(2,1)S(1)} %get-tuple-element.365), channel_id=1, source_target_pairs={{28,0},{0,4},{4,8},{8,12},{12,16},{16,20},{20,24},{24,28},{29,1},{... | collective-permute-start | bytes 393224 | tf_op jit(solution)/shard_map/while/body/ppermute | solution.py:28
